TPU v7x, 32 devices: a whole 2x2x4 slice. The times are simulated.
32 devices in a mesh: dp: 8 (over z, y), owner: 4 (over x, core).
Axes of the slice: x: 2, y: 2, z: 4, core: 2. Of those that a mesh axis runs over, the one named last changes fastest.
Arguments:
- grads: float32 [8, 32, 512, 128], P('dp', None, 'owner'), may hold values from -21 to 21
- momentum: float32 [64, 512, 128], P('dp', 'owner'), may hold values from -30 to 30
- slot_matrix: int32 [64], replicated, may hold values from -1 to 31, as said below
Outputs:
- updates: bfloat16 [32, 512, 128], P(None, 'owner')
- momentum_out: float32 [64, 512, 128], P('dp', 'owner')
Inputs may be any that keep to these rules, and one draw needn't show every extreme that they name: `slot_matrix`: entry s names the block held by slot s, or is -1 if slot s is empty; slots s with s // 8 == g belong to the owner group at index g of dp. Every one of the 32 blocks is held by exactly one slot, and some group, drawn from the seed, has all 8 slots filled.
All inputs are finite; a program needn't handle non-finite values.
Results may differ from a plain program's by a relative error of at most 0.038.
Values may be sent and summed in bfloat16 or wider, within the bound.
A program may use at most 64 MiB of HBM per device.

v0:
```python
import math
import jax
import jax.numpy as jnp
from jax import lax
from jax.sharding import PartitionSpec as P

C = 512
ITERS = 5
momentum_rate = 0.95
epsilon_norm = 1e-07
first_coef = 3.4445
third_coef = -4.775
fifth_coef = 2.0315


def local_gram(iterate):
    return jnp.einsum("kcr,kcq->krq", iterate, iterate, preferred_element_type=jnp.float32)


def make_poly(gram_matrix):
    square = jnp.einsum(
        "krq,kqp->krp", gram_matrix, gram_matrix, preferred_element_type=jnp.float32
    )
    return (third_coef * gram_matrix.astype(jnp.float32) + fifth_coef * square).astype(jnp.bfloat16)


def advance(iterate, polynomial):
    product = jnp.einsum("kcr,krq->kcq", iterate, polynomial, preferred_element_type=jnp.float32)
    return first_coef * iterate.astype(jnp.float32) + product


def whole_sweeps(iterate):
    for iteration in range(ITERS - 1):
        polynomial = make_poly(local_gram(iterate).astype(jnp.bfloat16))
        iterate = advance(iterate, polynomial).astype(jnp.bfloat16)
    return (iterate, make_poly(local_gram(iterate).astype(jnp.bfloat16)))


def finish(iterate, polynomial):
    return (math.sqrt(C) * advance(iterate, polynomial)).astype(jnp.bfloat16)


def local(grads, momentum, slot_matrix):
    partial_value = grads[0]
    present = (slot_matrix >= 0).astype(jnp.float32)
    picked = jnp.take(partial_value, jnp.maximum(slot_matrix, 0), axis=0) * present[:, None, None]
    summed = lax.psum_scatter(picked, "dp", scatter_dimension=0, tiled=True)
    renewed = momentum_rate * momentum + summed
    squares = lax.psum(jnp.sum(renewed * renewed, axis=(1, 2)), "owner")
    initial = (renewed / (jnp.sqrt(squares) + epsilon_norm)[:, None, None]).astype(jnp.bfloat16)
    iterate, polynomial = whole_sweeps(
        lax.all_to_all(initial, "owner", split_axis=0, concat_axis=1, tiled=True)
    )
    spread = finish(iterate, polynomial)
    update = lax.all_to_all(spread, "owner", split_axis=1, concat_axis=0, tiled=True)
    everyone = lax.all_gather(update, "dp", axis=0, tiled=True)
    all_slots = everyone.shape[0]
    matches = slot_matrix[None, :] == jnp.arange(grads.shape[1], dtype=jnp.int32)[:, None]
    slot_of = jnp.sum(
        jnp.where(matches, jnp.arange(all_slots, dtype=jnp.int32)[None, :], 0), axis=1
    )
    return (jnp.take(everyone, slot_of, axis=0), renewed)


def solution(mesh):
    return jax.shard_map(
        local,
        mesh=mesh,
        in_specs=(P("dp", None, "owner", None), P("dp", "owner", None), P()),
        out_specs=(P(None, "owner", None), P("dp", "owner", None)),
        check_vma=False,
    )
```

profile of v0, /device:TPU:0, one launch (start us, length us, event | category | flops | bytes accessed | tf_op | source)
XLA Modules:
  0.0 194.9 jit_solution(15638819623874804117)
XLA Ops:
  7.2 0.0 copy-start
  7.2 0.0 reduce-scatter.2.cloned.1.call-start
  7.2 0.8 broadcast_compare_fusion
  8.0 0.7 broadcast_maximum_fusion
  8.7 0.1 copy-done
  8.8 2.8 %gather_fusion = f32[64,128,128]{2,1,0:T(8,128)} fusion(f32[32,128,128]{2,1,0:T(8,128)S(1)} %bitcast.38, s32[1024]{0:T(1024)S(1)} %pad_clamp_fusion.1), kind=kCustom, calls=%fused_computation | custom fusion | bytes 8388864 | tf_op jit(solution)/shard_map/jit(_take)/gather | solution.py:46
  11.5 4.6 %select_multiply_fusion = f32[64,128,128]{2,1,0:T(8,128)} fusion(f32[64,128,128]{2,1,0:T(8,128)} %gather_fusion, f32[64]{0:T(128)S(1)} %get-tuple-element.5, pred[64]{0:T(512)(128)(4,1)S(1)} %get-tuple-element.4), kind=kLoop, calls=%fused_computation.2 | loop fusion | flops 2097152 | bytes 8388928 | tf_op jit(solution)/shard_map/mul | solution.py:46
  16.1 0.0 copy-start.2
  16.1 0.0 reduce-scatter.2.cloned.1.call-update
  16.1 0.0 all-gather.2.cloned.1.call-start
  16.2 91.1 %reduce-scatter.2.cloned.1.call-done = f32[8,128,128]{2,1,0:T(8,128)} async-done(((f32[64,128,128]{2,1,0:T(8,128)}), f32[8,128,128]{2,1,0:T(8,128)}) %reduce-scatter.2.cloned.1.call-update) | async-done | bytes 524304 | tf_op jit(solution)/shard_map/reduce_scatter | solution.py:47
  107.3 0.0 copy-done.2
  107.3 1.2 multiply_reduce_fusion
  108.5 0.0 copy-start.1
  108.5 6.2 %psum.7 = f32[8]{0:T(128)S(1)} all-reduce(f32[8]{0:T(128)S(1)} %get-tuple-element.2), channel_id=1, replica_groups=mesh['dp'=8,'owner'=4] {'owner'}, use_global_device_ids=true, to_apply=%region_3.4 | all-reduce | flops 8 | bytes 64 | tf_op jit(solution)/shard_map/psum | solution.py:49
  114.7 0.1 divide_convert_fusion
  114.8 8.4 %all_to_all.36 = bf16[8,128,128]{2,1,0:T(8,128)(2,1)S(1)} all-to-all(bf16[8,128,128]{2,1,0:T(8,128)(2,1)S(1)} %divide_convert_fusion), channel_id=1, replica_groups=mesh['dp'=8,'owner'=4] {'owner'}, dimensions={0} | all-to-all | bytes 524288 | tf_op jit(solution)/shard_map/all_to_all | solution.py:52
  123.2 0.0 copy-done.1
  123.3 0.3 convolution_convert_fusion.4
  123.5 0.0 copy-start.3
  123.5 0.4 fusion.2
  123.9 0.3 convolution_convert_fusion.3
  124.2 0.4 fusion.3
  124.6 0.3 convolution_convert_fusion.2
  124.8 0.4 fusion.4
  125.2 0.3 convolution_convert_fusion.1
  125.5 0.4 fusion.5
  125.9 0.3 convolution_convert_fusion
  126.1 0.4 fusion.1
  126.5 0.3 copy.40
  126.8 8.4 %all_to_all.37 = bf16[2,512,128]{2,0,1:T(2,128)(2,1)S(1)} all-to-all(bf16[2,512,128]{2,0,1:T(2,128)(2,1)S(1)} %copy.40), channel_id=1, replica_groups=mesh['dp'=8,'owner'=4] {'owner'}, dimensions={1} | all-to-all | bytes 524288 | tf_op jit(solution)/shard_map/all_to_all | solution.py:55
  135.2 0.7 copy.42
  135.9 0.0 all-gather.2.cloned.1.call-update
  136.0 0.0 copy-done.3
  136.0 0.1 select_reduce_fusion
  136.1 48.5 %all-gather.2.cloned.1.call-done = bf16[64,128,128]{2,1,0:T(8,128)(2,1)} async-done(((bf16[8,128,128]{2,1,0:T(8,128)(2,1)}), bf16[64,128,128]{2,1,0:T(8,128)(2,1)}) %all-gather.2.cloned.1.call-update) | async-done | bytes 2097168 | tf_op jit(solution)/shard_map/all_gather | solution.py:56
  184.6 2.3 %gather_fusion.1 = bf16[32,128,128]{2,1,0:T(8,128)(2,1)S(1)} fusion(bf16[64,128,128]{2,1,0:T(8,128)(2,1)} %all-gather.2.cloned.1.call-done, s32[1024]{0:T(1024)S(1)} %pad_clamp_fusion), kind=kCustom, calls=%fused_computation.1 | custom fusion | bytes 2097280 | tf_op jit(solution)/shard_map/jit(_take)/gather | solution.py:62
  186.9 1.1 broadcast_select_fusion
  (7 shorter events, 0.1 us)
Async XLA Ops:
  7.2 1.6 copy-start
  7.2 100.1 %reduce-scatter.2.cloned.1.call-start = ((), (), s32[]{:S(2)}) async-start(), calls=%async_computation.3 | async-start | bytes 4718592 | tf_op jit(solution)/shard_map/reduce_scatter | solution.py:47
  16.1 91.2 %copy-start.2 = (f32[8,128,128]{2,1,0:T(8,128)S(1)}, f32[8,128,128]{2,1,0:T(8,128)}, u32[]{:S(2)}) copy-start(f32[8,128,128]{2,1,0:T(8,128)} %param.4) | copy-start | bytes 1572868
  16.1 168.5 %all-gather.2.cloned.1.call-start = ((), (), s32[]{:S(2)}) async-start(), calls=%async_computation.4 | async-start | bytes 2359296 | tf_op jit(solution)/shard_map/all_gather | solution.py:56
  108.5 14.7 %copy-start.1 = (f32[8,128,128]{2,1,0:T(8,128)}, f32[8,128,128]{2,1,0:T(8,128)S(1)}, u32[]{:S(2)}) copy-start(f32[8,128,128]{2,1,0:T(8,128)S(1)} %get-tuple-element.3) | copy-start | bytes 1572868
  123.5 12.4 %copy-start.3 = (s32[64]{0:T(128)S(1)}, s32[64]{0:T(128)}, u32[]{:S(2)}) copy-start(s32[64]{0:T(128)} %param.5) | copy-start | bytes 772
Sparse Core Ops, SparseCore 0:
  16.2 91.0 reduce-scatter.1
  136.1 48.4 all-gather.1
where the time goes:
time: 195 us
  waiting for transfers between devices  140 us (72%)
  blocking collectives  23 us (12%)
  between operations  14.2 us (7%)
  other arithmetic  8.63 us (4%)
  local copies, waits for them, and re-layouts  6.24 us (3%)
  matrix products  3.19 us (2%)
    reduce_scatter x1, waiting for transfers between devices, local(): summed = lax.psum_scatter(picked, 'dp', scatter_dimension=0, tiled=True)  91.1 us
    all_gather x1, waiting for transfers between devices, local(): everyone = lax.all_gather(update, 'dp', axis=0, tiled=True)  48.5 us
    all_to_all x1, blocking collectives, local(): lax.all_to_all(initial, 'owner', split_axis=0, concat_axis=1, tiled=True)  8.39 us
    all_to_all x1, blocking collectives, local(): lax.all_to_all(spread, 'owner', split_axis=1, concat_axis=0, tiled=True)  8.39 us
    psum x1, blocking collectives, local(): squares = lax.psum(jnp.sum(renewed * renewed, axis=(1, 2)), 'owner')  6.2 us
    mul x1, other arithmetic, local(): jnp.take(partial_value, jnp.maximum(slot_matrix, 0), axis=0)  4.55 us
  transfers between devices with their start and end apart: 2, of which 2 were waited for; matrix products, arithmetic and copies ran while one was open for 0% of the time, Pallas kernels for 0%

commit v1 on v0

--- a/solution.py
+++ b/solution.py
@@ -53,7 +53,12 @@
     )
     spread = finish(iterate, polynomial)
     update = lax.all_to_all(spread, "owner", split_axis=1, concat_axis=0, tiled=True)
-    everyone = lax.all_gather(update, "dp", axis=0, tiled=True)
+    ring = [update]
+    for hop in range(7):
+        ring.append(lax.ppermute(ring[-1], "dp", [(dev, (dev + 1) % 8) for dev in range(8)]))
+    everyone = jnp.roll(
+        jnp.concatenate(ring[::-1], axis=0), (lax.axis_index("dp") + 1) * ring[0].shape[0], axis=0
+    )
     all_slots = everyone.shape[0]
     matches = slot_matrix[None, :] == jnp.arange(grads.shape[1], dtype=jnp.int32)[:, None]
     slot_of = jnp.sum(

time: 195 us -> 221 us (1.13)
  waiting for transfers between devices: 140 us -> 157 us
  local copies, waits for them, and re-layouts: 6.24 us -> 13 us
    ppermute x0 -> x7, waiting for transfers between devices: none -> 65.4 us  [local(): lax.ppermute(ring[-1], 'dp', [(dev, (dev + 1) % 8) for dev in range(8)])]
    all_gather x1 -> x0, waiting for transfers between devices: 48.5 us -> none  [local(): everyone = lax.all_gather(update, 'dp', axis=0, tiled=True)]
    unnamed x8 -> x25, local copies, waits for them, and re-layouts: 0.1 us -> 6 us
  transfers between devices with their start and end apart: 2 -> 8, of which waited for: 2 -> 8; matrix products, arithmetic and copies ran while one was open for 0% -> 0% of each run, Pallas kernels for 0% -> 0%
where the time goes in v1:
time: 221 us
  waiting for transfers between devices  157 us (71%)
  blocking collectives  23 us (10%)
  between operations  14.3 us (6%)
  local copies, waits for them, and re-layouts  13 us (6%)
  other arithmetic  9.29 us (4%)
  matrix products  3.2 us (1%)
    reduce_scatter x1, waiting for transfers between devices, local(): summed = lax.psum_scatter(picked, 'dp', scatter_dimension=0, tiled=True)  91.2 us
    ppermute x7, waiting for transfers between devices, local(): lax.ppermute(ring[-1], 'dp', [(dev, (dev + 1) % 8) for dev in range(8)])  65.4 us
    all_to_all x1, blocking collectives, local(): lax.all_to_all(initial, 'owner', split_axis=0, concat_axis=1, tiled=True)  8.39 us
    all_to_all x1, blocking collectives, local(): lax.all_to_all(spread, 'owner', split_axis=1, concat_axis=0, tiled=True)  8.39 us
    psum x1, blocking collectives, local(): squares = lax.psum(jnp.sum(renewed * renewed, axis=(1, 2)), 'owner')  6.2 us
    unnamed x25, local copies, waits for them, and re-layouts  6 us
    mul x1, other arithmetic, local(): jnp.take(partial_value, jnp.maximum(slot_matrix, 0), axis=0)  4.56 us
  transfers between devices with their start and end apart: 8, of which 8 were waited for; matrix products, arithmetic and copies ran while one was open for 0% of the time, Pallas kernels for 0%

profile of v1, /device:TPU:0, one launch (start us, length us, event | category | flops | bytes accessed | tf_op | source)
XLA Modules:
  0.0 220.9 jit_solution(4572982670919440507)
XLA Ops:
  7.2 0.0 copy-start
  7.2 0.0 reduce-scatter.2.cloned.1.call-start
  7.2 0.9 select_reduce_fusion
  8.1 0.7 broadcast_maximum_fusion
  8.8 0.7 broadcast_compare_fusion
  9.5 0.0 copy-done
  9.5 2.8 %gather_fusion = f32[64,128,128]{2,1,0:T(8,128)} fusion(f32[32,128,128]{2,1,0:T(8,128)S(1)} %bitcast.38, s32[1024]{0:T(1024)S(1)} %get-tuple-element.7), kind=kCustom, calls=%fused_computation | custom fusion | bytes 8388864 | tf_op jit(solution)/shard_map/jit(_take)/gather | solution.py:46
  12.2 4.6 %select_multiply_fusion = f32[64,128,128]{2,1,0:T(8,128)} fusion(f32[64,128,128]{2,1,0:T(8,128)} %gather_fusion, f32[64]{0:T(128)S(1)} %get-tuple-element.5, pred[64]{0:T(512)(128)(4,1)S(1)} %get-tuple-element.4), kind=kLoop, calls=%fused_computation.2 | loop fusion | flops 2097152 | bytes 8388928 | tf_op jit(solution)/shard_map/mul | solution.py:46
  16.8 0.0 copy-start.4
  16.8 0.0 reduce-scatter.2.cloned.1.call-update
  16.8 91.2 %reduce-scatter.2.cloned.1.call-done = f32[8,128,128]{2,1,0:T(8,128)} async-done(((f32[64,128,128]{2,1,0:T(8,128)}), f32[8,128,128]{2,1,0:T(8,128)}) %reduce-scatter.2.cloned.1.call-update) | async-done | bytes 524304 | tf_op jit(solution)/shard_map/reduce_scatter | solution.py:47
  108.0 0.0 copy-done.4
  108.0 1.2 multiply_reduce_fusion
  109.2 0.0 copy-start.1
  109.2 6.2 %psum.7 = f32[8]{0:T(128)S(1)} all-reduce(f32[8]{0:T(128)S(1)} %get-tuple-element.2), channel_id=1, replica_groups=mesh['dp'=8,'owner'=4] {'owner'}, use_global_device_ids=true, to_apply=%region_3.4 | all-reduce | flops 8 | bytes 64 | tf_op jit(solution)/shard_map/psum | solution.py:49
  115.4 0.1 divide_convert_fusion
  115.6 8.4 %all_to_all.36 = bf16[8,128,128]{2,1,0:T(8,128)(2,1)S(1)} all-to-all(bf16[8,128,128]{2,1,0:T(8,128)(2,1)S(1)} %divide_convert_fusion), channel_id=1, replica_groups=mesh['dp'=8,'owner'=4] {'owner'}, dimensions={0} | all-to-all | bytes 524288 | tf_op jit(solution)/shard_map/all_to_all | solution.py:52
  124.0 0.0 copy-done.1
  124.0 0.3 convolution_convert_fusion.4
  124.3 0.4 fusion.2
  124.6 0.3 convolution_convert_fusion.3
  124.9 0.4 fusion.3
  125.3 0.3 convolution_convert_fusion.2
  125.5 0.4 fusion.4
  125.9 0.3 convolution_convert_fusion.1
  126.2 0.4 fusion.5
  126.6 0.3 convolution_convert_fusion
  126.8 0.4 fusion.1
  127.2 0.3 copy.40
  127.5 8.4 %all_to_all.37 = bf16[2,512,128]{2,0,1:T(2,128)(2,1)S(1)} all-to-all(bf16[2,512,128]{2,0,1:T(2,128)(2,1)S(1)} %copy.40), channel_id=1, replica_groups=mesh['dp'=8,'owner'=4] {'owner'}, dimensions={1} | all-to-all | bytes 524288 | tf_op jit(solution)/shard_map/all_to_all | solution.py:55
  136.0 1.5 collective-permute-start
  137.5 8.9 %collective-permute-done = bf16[8,128,128]{2,1,0:T(8,128)(2,1)S(1)} collective-permute-done((bf16[8,128,128]{2,1,0:T(8,128)(2,1)S(1)}, bf16[8,128,128]{2,1,0:T(8,128)(2,1)S(1)}, u32[]{:S(2)}, u32[]{:S(2)}) %collective-permute-start) | collective-permute-done | bytes 262176 | tf_op jit(solution)/shard_map/ppermute | solution.py:58
  146.4 0.0 collective-permute-start.1
  146.4 9.5 %collective-permute-done.1 = bf16[8,128,128]{2,1,0:T(8,128)(2,1)S(1)} collective-permute-done((bf16[8,128,128]{2,1,0:T(8,128)(2,1)S(1)}, bf16[8,128,128]{2,1,0:T(8,128)(2,1)S(1)}, u32[]{:S(2)}, u32[]{:S(2)}) %collective-permute-start.1) | collective-permute-done | bytes 262176 | tf_op jit(solution)/shard_map/ppermute | solution.py:58
  155.9 0.0 collective-permute-start.2
  155.9 9.1 %collective-permute-done.2 = bf16[8,128,128]{2,1,0:T(8,128)(2,1)S(1)} collective-permute-done((bf16[8,128,128]{2,1,0:T(8,128)(2,1)S(1)}, bf16[8,128,128]{2,1,0:T(8,128)(2,1)S(1)}, u32[]{:S(2)}, u32[]{:S(2)}) %collective-permute-start.2) | collective-permute-done | bytes 262176 | tf_op jit(solution)/shard_map/ppermute | solution.py:58
  165.0 0.0 collective-permute-start.3
  165.0 9.1 %collective-permute-done.3 = bf16[8,128,128]{2,1,0:T(8,128)(2,1)S(1)} collective-permute-done((bf16[8,128,128]{2,1,0:T(8,128)(2,1)S(1)}, bf16[8,128,128]{2,1,0:T(8,128)(2,1)S(1)}, u32[]{:S(2)}, u32[]{:S(2)}) %collective-permute-start.3) | collective-permute-done | bytes 262176 | tf_op jit(solution)/shard_map/ppermute | solution.py:58
  174.0 0.0 collective-permute-start.4
  174.0 9.1 %collective-permute-done.4 = bf16[8,128,128]{2,1,0:T(8,128)(2,1)S(1)} collective-permute-done((bf16[8,128,128]{2,1,0:T(8,128)(2,1)S(1)}, bf16[8,128,128]{2,1,0:T(8,128)(2,1)S(1)}, u32[]{:S(2)}, u32[]{:S(2)}) %collective-permute-start.4) | collective-permute-done | bytes 262176 | tf_op jit(solution)/shard_map/ppermute | solution.py:58
  183.1 0.0 copy-start.2
  183.1 0.7 copy-done.2
  183.8 0.0 collective-permute-start.5
  183.8 10.4 %collective-permute-done.5 = bf16[8,128,128]{2,1,0:T(8,128)(2,1)} collective-permute-done((bf16[8,128,128]{2,1,0:T(8,128)(2,1)S(1)}, bf16[8,128,128]{2,1,0:T(8,128)(2,1)}, u32[]{:S(2)}, u32[]{:S(2)}) %collective-permute-start.5) | collective-permute-done | bytes 262176 | tf_op jit(solution)/shard_map/ppermute | solution.py:58
  194.2 0.0 collective-permute-start.6
  194.2 0.0 copy-start.3
  194.2 9.4 %collective-permute-done.6 = bf16[8,128,128]{2,1,0:T(8,128)(2,1)} collective-permute-done((bf16[8,128,128]{2,1,0:T(8,128)(2,1)}, bf16[8,128,128]{2,1,0:T(8,128)(2,1)}, u32[]{:S(2)}, u32[]{:S(2)}) %collective-permute-start.6) | collective-permute-done | bytes 262176 | tf_op jit(solution)/shard_map/ppermute | solution.py:58
  203.6 1.0 constant_dynamic-update-slice_fusion.15
  204.6 1.0 constant_dynamic-update-slice_fusion.14
  205.6 1.0 constant_dynamic-update-slice_fusion.13
  206.8 1.0 constant_dynamic-update-slice_fusion.7
  207.8 1.0 constant_dynamic-update-slice_fusion.6
  208.8 0.0 copy-done.3
  209.0 1.5 constant_dynamic-slice_fusion
  210.5 2.3 %gather_fusion.1 = bf16[32,128,128]{2,1,0:T(8,128)(2,1)S(1)} fusion(bf16[64,128,128]{2,1,0:T(8,128)(2,1)} %constant_dynamic-slice_fusion, s32[1024]{0:T(1024)S(1)} %get-tuple-element.6), kind=kCustom, calls=%fused_computation.1 | custom fusion | bytes 2097280 | tf_op jit(solution)/shard_map/jit(_take)/gather | solution.py:67
  212.9 1.1 broadcast_select_fusion
  (18 shorter events, 0.5 us)
Async XLA Ops:
  7.2 2.3 %copy-start = (f32[1,32,128,128]{3,2,1,0:T(8,128)S(1)}, f32[1,32,128,128]{3,2,1,0:T(8,128)}, u32[]{:S(2)}) copy-start(f32[1,32,128,128]{3,2,1,0:T(8,128)} %param.3) | copy-start | bytes 6291460
  7.2 100.8 %reduce-scatter.2.cloned.1.call-start = ((), (), s32[]{:S(2)}) async-start(), calls=%async_computation.3 | async-start | bytes 4718592 | tf_op jit(solution)/shard_map/reduce_scatter | solution.py:47
  16.8 91.2 %copy-start.4 = (f32[8,128,128]{2,1,0:T(8,128)S(1)}, f32[8,128,128]{2,1,0:T(8,128)}, u32[]{:S(2)}) copy-start(f32[8,128,128]{2,1,0:T(8,128)} %param.4) | copy-start | bytes 1572868
  109.2 14.7 %copy-start.1 = (f32[8,128,128]{2,1,0:T(8,128)}, f32[8,128,128]{2,1,0:T(8,128)S(1)}, u32[]{:S(2)}) copy-start(f32[8,128,128]{2,1,0:T(8,128)S(1)} %get-tuple-element.3) | copy-start | bytes 1572868
  136.0 10.4 %collective-permute-start = (bf16[8,128,128]{2,1,0:T(8,128)(2,1)S(1)}, bf16[8,128,128]{2,1,0:T(8,128)(2,1)S(1)}, u32[]{:S(2)}, u32[]{:S(2)}) collective-permute-start(bf16[8,128,128]{2,1,0:T(8,128)(2,1)S(1)} %bitcast.41), channel_id=1, source_target_pairs={{0,4},{4,8},{8,12},{12,16},{16,20},{20,24},{24,28},{28,0},{1,5},{5... | collective-permute-start | bytes 786440 | tf_op jit(solution)/shard_map/ppermute | solution.py:58
  146.4 9.5 %collective-permute-start.1 = (bf16[8,128,128]{2,1,0:T(8,128)(2,1)S(1)}, bf16[8,128,128]{2,1,0:T(8,128)(2,1)S(1)}, u32[]{:S(2)}, u32[]{:S(2)}) collective-permute-start(bf16[8,128,128]{2,1,0:T(8,128)(2,1)S(1)} %collective-permute-done), channel_id=1, source_target_pairs={{0,4},{4,8},{8,12},{12,16},{16,20},{20,24},{24,28},{28,0},{1,5},{5... | collective-permute-start | bytes 786440 | tf_op jit(solution)/shard_map/ppermute | solution.py:58
  155.9 9.1 %collective-permute-start.2 = (bf16[8,128,128]{2,1,0:T(8,128)(2,1)S(1)}, bf16[8,128,128]{2,1,0:T(8,128)(2,1)S(1)}, u32[]{:S(2)}, u32[]{:S(2)}) collective-permute-start(bf16[8,128,128]{2,1,0:T(8,128)(2,1)S(1)} %collective-permute-done.1), channel_id=1, source_target_pairs={{0,4},{4,8},{8,12},{12,16},{16,20},{20,24},{24,28},{28,0},{1,5},{5... | collective-permute-start | bytes 786440 | tf_op jit(solution)/shard_map/ppermute | solution.py:58
  165.0 9.1 %collective-permute-start.3 = (bf16[8,128,128]{2,1,0:T(8,128)(2,1)S(1)}, bf16[8,128,128]{2,1,0:T(8,128)(2,1)S(1)}, u32[]{:S(2)}, u32[]{:S(2)}) collective-permute-start(bf16[8,128,128]{2,1,0:T(8,128)(2,1)S(1)} %collective-permute-done.2), channel_id=1, source_target_pairs={{0,4},{4,8},{8,12},{12,16},{16,20},{20,24},{24,28},{28,0},{1,5},{5... | collective-permute-start | bytes 786440 | tf_op jit(solution)/shard_map/ppermute | solution.py:58
  174.0 9.1 %collective-permute-start.4 = (bf16[8,128,128]{2,1,0:T(8,128)(2,1)S(1)}, bf16[8,128,128]{2,1,0:T(8,128)(2,1)S(1)}, u32[]{:S(2)}, u32[]{:S(2)}) collective-permute-start(bf16[8,128,128]{2,1,0:T(8,128)(2,1)S(1)} %collective-permute-done.3), channel_id=1, source_target_pairs={{0,4},{4,8},{8,12},{12,16},{16,20},{20,24},{24,28},{28,0},{1,5},{5... | collective-permute-start | bytes 786440 | tf_op jit(solution)/shard_map/ppermute | solution.py:58
  183.1 0.7 copy-start.2
  183.8 10.4 %collective-permute-start.5 = (bf16[8,128,128]{2,1,0:T(8,128)(2,1)S(1)}, bf16[8,128,128]{2,1,0:T(8,128)(2,1)}, u32[]{:S(2)}, u32[]{:S(2)}) collective-permute-start(bf16[8,128,128]{2,1,0:T(8,128)(2,1)S(1)} %collective-permute-done.4), channel_id=1, source_target_pairs={{0,4},{4,8},{8,12},{12,16},{16,20},{20,24},{24,28},{28,0},{1,5},{5... | collective-permute-start | bytes 786440 | tf_op jit(solution)/shard_map/ppermute | solution.py:58
  194.2 9.4 %collective-permute-start.6 = (bf16[8,128,128]{2,1,0:T(8,128)(2,1)}, bf16[8,128,128]{2,1,0:T(8,128)(2,1)}, u32[]{:S(2)}, u32[]{:S(2)}) collective-permute-start(bf16[8,128,128]{2,1,0:T(8,128)(2,1)} %collective-permute-done.5), channel_id=1, source_target_pairs={{0,4},{4,8},{8,12},{12,16},{16,20},{20,24},{24,28},{28,0},{1,5},{5... | collective-permute-start | bytes 786440 | tf_op jit(solution)/shard_map/ppermute | solution.py:58
  194.2 14.5 %copy-start.3 = (bf16[8,128,128]{2,1,0:T(8,128)(2,1)S(1)}, bf16[8,128,128]{2,1,0:T(8,128)(2,1)}, u32[]{:S(2)}) copy-start(bf16[8,128,128]{2,1,0:T(8,128)(2,1)} %copy-done.2) | copy-start | bytes 786436
Sparse Core Ops, SparseCore 0:
  16.9 91.0 reduce-scatter.1
